TPU v7x, 256 devices: a whole 4x4x8 slice. The times are simulated.
256 devices in a mesh: row: 8 (over z), col: 32 (over x, y, core).
Axes of the slice: x: 4, y: 4, z: 8, core: 2. Of those that a mesh axis runs over, the one named last changes fastest.
Arguments:
- rho_real: float32 [4096, 4096], P('row', 'col'), may hold values from -2.5 to 4, as said below
- rho_imag: float32 [4096, 4096], P('row', 'col'), may hold values from -2.5 to 2.5, as said below
- hamiltonian: bfloat16 [4096, 4096], P('row', 'col'), may hold values from -1 to 1
- amplitudes: float32 [8, 4096], replicated, may hold values from 0.15 to 0.6
- offsets: int32 [8], replicated, may hold values from -16 to 16
- active_jumps: int32 [1], replicated, may hold values from 4 to 8
Outputs:
- rho_next_real: float32 [4096, 4096], P('row', 'col')
- rho_next_imag: float32 [4096, 4096], P('row', 'col')
Inputs may be any that keep to these rules, and one draw needn't show every extreme that they name: `rho_real`: symmetric, with every diagonal entry 0.5 or more. `rho_imag`: antisymmetric.
All inputs are finite; a program needn't handle non-finite values.
Results may differ from a plain program's by a relative error of at most 0.001.
Values may be sent and summed in bfloat16 or wider, within the bound.
A program may use at most 64 MiB of HBM per device.

v0:
```python
import jax
import jax.numpy as jnp
from jax import lax
from jax.sharding import Mesh
from jax.sharding import PartitionSpec as P

OMAX = 16
COL = ("col_0", "col_1", "col_2")
ROW_COL = ("row", "col_0", "col_1", "col_2")
step_size = 0.25


def in_order(tiles, dim):
    lengths = list(tiles.shape[1:])
    lengths[dim] *= tiles.shape[0]
    return jnp.moveaxis(tiles, 0, dim).reshape(lengths)


def sent_to_all(x, axis):
    peers = lax.axis_size(axis)
    return lax.all_to_all(jnp.broadcast_to(x[None], (peers, *x.shape)), axis, 0, 0, tiled=True)


def gathered_copies(x, axis, dim):
    return in_order(sent_to_all(x, axis), dim)


def by_axis(x, axes):
    for axis in axes:
        x = lax.psum(x, axis)
    return x


def in_one_piece(arrays, axis, dim, along):
    both = jnp.concatenate(arrays, axis=along)
    out, at, finished = (gathered_copies(both, axis, dim), 0, [])
    for a in arrays:
        finished.append(lax.slice_in_dim(out, at, at + a.shape[along], axis=along))
        at += a.shape[along]
    return tuple(finished)


def sent_together(arrays, axis, dim, along):
    both = jnp.concatenate(arrays, axis=along)
    out, at, finished = (lax.all_gather(both, axis, axis=dim, tiled=True), 0, [])
    for a in arrays:
        finished.append(lax.slice_in_dim(out, at, at + a.shape[along], axis=along))
        at += a.shape[along]
    return tuple(finished)


def extended(cells, sides, width):
    for axis, dim in sides:
        count = lax.axis_size(axis)
        ends = count - 1
        head = lax.slice_in_dim(cells, 0, width, axis=dim)
        tail = lax.slice_in_dim(cells, cells.shape[dim] - width, cells.shape[dim], axis=dim)
        cells = jnp.concatenate(
            [
                lax.ppermute(tail, axis, [(i, (i + 1) % count) for i in range(ends)]),
                cells,
                lax.ppermute(head, axis, [((i + 1) % count, i) for i in range(ends)]),
            ],
            axis=dim,
        )
    return cells


def dissipate(matrix, padded, amplitudes, offsets, active, row_first, col_first):
    height = matrix.shape[1]
    breadth = matrix.shape[2]
    levels = amplitudes.shape[1]
    margin = (padded.shape[1] - height) // 2
    positions = jnp.arange(levels, dtype=jnp.int32)
    summed = jnp.zeros(matrix.shape, matrix.dtype)
    for jump_slot in range(amplitudes.shape[0]):
        offset = offsets[jump_slot]
        inside = (positions + offset >= 0) & (positions + offset < levels)
        strength = jnp.where(inside, amplitudes[jump_slot], 0.0)
        outflow = jnp.pad(strength * strength, (margin, margin))
        outflow = lax.dynamic_slice_in_dim(outflow, margin - offset, levels)
        row_strength = lax.dynamic_slice_in_dim(strength, row_first, height)
        col_strength = lax.dynamic_slice_in_dim(strength, col_first, breadth)
        row_outflow = lax.dynamic_slice_in_dim(outflow, row_first, height)
        col_outflow = lax.dynamic_slice_in_dim(outflow, col_first, breadth)
        corner = margin + offset
        shifted = lax.dynamic_slice(padded, (jnp.int32(0), corner, corner), (2, height, breadth))
        contribution = (
            row_strength[:, None] * col_strength[None, :] * shifted
            - 0.5 * (row_outflow[:, None] + col_outflow[None, :]) * matrix
        )
        summed = summed + jnp.where(jump_slot < active, contribution, 0.0)
    return summed


def diagonal_sum(matrix, row_first, col_first):
    row_index = lax.broadcasted_iota(jnp.int32, matrix.shape, 0) + row_first
    col_index = lax.broadcasted_iota(jnp.int32, matrix.shape, 1) + col_first
    return jnp.sum(jnp.where(row_index == col_index, matrix, 0.0))


def local(rho_real, rho_imag, hamiltonian, amplitudes, offsets, active_jumps):
    height, breadth = rho_real.shape
    levels = amplitudes.shape[1]
    row_first = lax.axis_index("row") * height
    col_first = lax.axis_index(COL) * breadth
    active = active_jumps[0]
    ham_columns = gathered_copies(hamiltonian, "row", 0)
    start_trace = by_axis(diagonal_sum(rho_real, row_first, col_first), ROW_COL)

    def drift(real_part, imag_part):
        real_low = real_part.astype(jnp.bfloat16)
        imag_low = imag_part.astype(jnp.bfloat16)
        row_panel = lax.all_gather(hamiltonian, COL, axis=1, tiled=True)
        pieces = in_one_piece((real_low, imag_low), "row", 0, 1)
        strip = row_panel
        left_real = jnp.dot(strip, pieces[0], preferred_element_type=jnp.float32)
        left_imag = jnp.dot(strip, pieces[1], preferred_element_type=jnp.float32)
        pieces = sent_together((real_low, imag_low), COL, 1, 0)
        strip = ham_columns
        right_real = jnp.dot(pieces[0], strip, preferred_element_type=jnp.float32)
        right_imag = jnp.dot(pieces[1], strip, preferred_element_type=jnp.float32)
        matrix = jnp.stack([real_part, imag_part])
        padded = extended(matrix.astype(jnp.bfloat16), (("row", 1), (COL, 2)), OMAX).astype(
            matrix.dtype
        )
        loss = dissipate(matrix, padded, amplitudes, offsets, active, row_first, col_first)
        return (left_imag - right_imag + loss[0], right_real - left_real + loss[1])

    first_real, first_imag = drift(rho_real, rho_imag)
    middle_real = rho_real + step_size * first_real
    middle_imag = rho_imag + step_size * first_imag
    rescale = levels / start_trace
    middle_real = middle_real * rescale
    middle_imag = middle_imag * rescale
    second_real, second_imag = drift(middle_real, middle_imag)
    updated_real = rho_real + 0.5 * step_size * (first_real + second_real)
    updated_imag = rho_imag + 0.5 * step_size * (first_imag + second_imag)
    rescale = levels / start_trace
    return (updated_real * rescale, updated_imag * rescale)


def solution(mesh):
    split = Mesh(
        mesh.devices.reshape(mesh.shape["row"], 4, 4, 2), ("row", "col_0", "col_1", "col_2")
    )
    placed = (P("row", COL), P("row", COL), P("row", COL), P(), P(), P())
    return jax.shard_map(
        local,
        mesh=split,
        in_specs=placed,
        out_specs=(P("row", COL), P("row", COL)),
        check_vma=False,
    )
```

profile of v0, /device:TPU:25, one launch (start us, length us, event | category | flops | bytes accessed | tf_op | source)
XLA Modules:
  0.0 268.6 jit_solution(7100053074104402569)
XLA Ops:
  7.3 1.0 convert_element_type.42
  8.2 1.8 select_reduce_fusion
  10.0 0.7 pad_maximum_fusion.3
  10.8 0.7 all-gather.4.cloned.1.call-update
  11.5 1.1 copy.16
  12.6 1.1 copy.10
  13.7 0.7 fusion.83
  14.4 3.5 %collective-permute-start = (bf16[2,16,128]{1,2,0:T(8,128)(2,1)}, bf16[2,16,128]{1,2,0:T(8,128)(2,1)S(1)}, u32[]{:S(2)}, u32[]{:S(2)}) collective-permute-start(bf16[2,16,128]{1,2,0:T(8,128)(2,1)} %get-tuple-element.32), channel_id=1, source_target_pairs={{0,32},{32,64},{64,96},{96,128},{128,160},{160,192},{192,224},{1,3... | collective-permute-start | bytes 24584 | tf_op jit(solution)/shard_map/ppermute | solution.py:60
  18.0 1.3 collective-permute-start.1
  19.3 2.0 broadcast_in_dim.49
  21.3 9.8 %all-to-all-start.1 = ((bf16[8,512,128]{2,1,0:T(8,128)(2,1)}), bf16[8,512,128]{2,1,0:T(8,128)(2,1)S(1)}, u32[]{:S(2)}, u32[]{:S(2)}) async-start(bf16[8,512,128]{2,1,0:T(8,128)(2,1)} %broadcast_in_dim.49), calls=%async_computation.1 | async-start | bytes 2097152 | tf_op jit(solution)/shard_map/all_to_all | solution.py:21
  31.1 0.7 fusion.85
  34.6 0.6 fusion.76
  35.9 0.7 fusion.66
  37.1 0.7 fusion.70
  38.4 27.6 %psum.28 = f32[]{:T(128)} all-reduce(f32[]{:T(128)} %get-tuple-element.30), channel_id=1, replica_groups=mesh['row'=8,'col_0'=4,'col_1'=4,'col_2'=2] {'row'}, use_global_device_ids=true, to_apply=%region_1.2 | all-reduce | flops 1 | bytes 8 | tf_op jit(solution)/shard_map/psum | solution.py:30
  72.4 0.7 pad_dynamic-slice_fusion.8
  73.0 0.7 pad_dynamic-slice_fusion.10
  74.3 0.7 pad_dynamic-slice_fusion.12
  75.0 0.6 fusion.80
  76.2 0.7 pad_dynamic-slice_fusion.5
  76.9 0.7 pad_dynamic-slice_fusion.15
  77.5 0.7 pad_dynamic-slice_fusion.9
  79.4 1.5 broadcast_in_dim.48
  81.1 4.2 %all-to-all-start = ((bf16[8,512,256]{2,1,0:T(8,128)(2,1)}), bf16[8,512,256]{2,1,0:T(8,128)(2,1)S(1)}, u32[]{:S(2)}, u32[]{:S(2)}) async-start(bf16[8,512,256]{2,1,0:T(8,128)(2,1)} %broadcast_in_dim.48), calls=%async_computation | async-start | bytes 4194304 | tf_op jit(solution)/shard_map/all_to_all | solution.py:21
  85.9 9.1 %psum.29 = f32[]{:T(128)} all-reduce(f32[]{:T(128)} %psum.28), channel_id=1, replica_groups=mesh['row'=8,'col_0'=4,'col_1'=4,'col_2'=2] {'col_0'}, use_global_device_ids=true, to_apply=%region_2.3 | all-reduce | flops 1 | bytes 8 | tf_op jit(solution)/shard_map/psum | solution.py:30
  97.6 0.7 pad_dynamic-slice_fusion.7
  98.4 1.5 add_multiply_fusion.2
  99.9 0.9 broadcast_multiply_fusion.6
  100.8 1.6 add_multiply_fusion.8
  102.4 0.9 broadcast_multiply_fusion.4
  103.3 1.6 add_multiply_fusion.6
  104.9 0.9 broadcast_multiply_fusion.2
  106.4 6.6 %psum.30 = f32[]{:T(128)} all-reduce(f32[]{:T(128)} %psum.29), channel_id=1, replica_groups=mesh['row'=8,'col_0'=4,'col_1'=4,'col_2'=2] {'col_1'}, use_global_device_ids=true, to_apply=%region_3.4 | all-reduce | flops 1 | bytes 8 | tf_op jit(solution)/shard_map/psum | solution.py:30
  113.0 0.7 pad_maximum_fusion.11
  113.7 11.7 %collective-permute-start.2 = (bf16[2,544,16]{1,2,0:T(8,128)(2,1)}, bf16[2,544,16]{1,2,0:T(8,128)(2,1)}, u32[]{:S(2)}, u32[]{:S(2)}) collective-permute-start(bf16[2,544,16]{1,2,0:T(8,128)(2,1)} %get-tuple-element.26), channel_id=1, source_target_pairs={{0,1},{1,2},{2,3},{3,4},{4,5},{5,6},{6,7},{7,8},{8,9},{9,10},{10,1... | collective-permute-start | bytes 104456 | tf_op jit(solution)/shard_map/ppermute | solution.py:60
  125.4 1.9 collective-permute-start.3
  127.3 1.6 add_multiply_fusion.4
  128.9 3.2 %psum.31 = f32[]{:T(128)} all-reduce(f32[]{:T(128)} %psum.30), channel_id=1, replica_groups=mesh['row'=8,'col_0'=4,'col_1'=4,'col_2'=2] {'col_2'}, use_global_device_ids=true, to_apply=%region_4.5 | all-reduce | flops 1 | bytes 8 | tf_op jit(solution)/shard_map/psum | solution.py:30
  148.6 1.0 maximum_convert_fusion
  149.5 4.5 %select_add_fusion.1 = f32[2,512,128]{1,2,0:T(8,128)} fusion(f32[2,544,160]{1,2,0:T(8,128)S(1)} %maximum_convert_fusion, s32[]{:T(128)S(6)} %select_n.358, s32[]{:T(128)S(6)} %select_n.359, s32[]{:T(128)S(6)} %select_n.351, s32[]{:T(128)S(6)} %select_n.352, s32[]{:T(128)S(6)} %select_n.344, s32[]{:T(128)S(6)} %select_n.345, s32[]{:T(128)S(6)} %select_n.337, ...), kind=kLoop, calls=%fused_computation.35 | loop fusion | flops 5242880 | bytes 9437256 | tf_op jit(solution)/shard_map/add | solution.py:92
  154.1 4.0 %fusion.6 = f32[512,128]{0,1:T(8,128)S(1)} fusion(bf16[4096,128]{1,0:T(8,128)(2,1)} %bitcast.105, bf16[1024,4096]{1,0:T(8,128)(2,1)} %all-gather.6.cloned.1.call-done), kind=kOutput, calls=%fused_computation.6 | convolution fusion | flops 536870912 | bytes 5505024 | tf_op jit(solution)/shard_map/dot_general | solution.py:122
  158.1 3.8 %fusion.9 = f32[512,128]{0,1:T(8,128)S(1)} fusion(f32[512,128]{0,1:T(8,128)S(1)} %fusion.6, bf16[512,4096]{1,0:T(8,128)(2,1)} %all-gather.4.cloned.1.call-done, bf16[4096,256]{1,0:T(8,128)(2,1)S(1)} %bitcast.97, f32[2,512,128]{1,2,0:T(8,128)} %select_add_fusion.1), kind=kOutput, calls=%fused_computation.13 | convolution fusion | flops 537001984 | bytes 6029312 | tf_op jit(solution)/shard_map/dot_general | solution.py:118
  162.0 0.7 copy-done.5
  162.8 3.8 %fusion.4 = f32[512,128]{0,1:T(8,128)S(1)} fusion(bf16[4096,128]{1,0:T(8,128)(2,1)S(1)} %bitcast.108, bf16[1024,4096]{1,0:T(8,128)(2,1)} %all-gather.6.cloned.1.call-done), kind=kOutput, calls=%fused_computation.4 | convolution fusion | flops 536870912 | bytes 5505024 | tf_op jit(solution)/shard_map/dot_general | solution.py:121
  166.6 1.5 fusion.11
  168.2 0.7 copy-done.3
  168.9 0.7 pad_maximum_fusion.5
  169.9 1.4 broadcast_in_dim.53
  171.3 6.9 %all-to-all-start.2 = ((bf16[8,512,256]{2,1,0:T(8,128)(2,1)}), bf16[8,512,256]{2,1,0:T(8,128)(2,1)S(1)}, u32[]{:S(2)}, u32[]{:S(2)}) async-start(bf16[8,512,256]{2,1,0:T(8,128)(2,1)} %broadcast_in_dim.53), calls=%async_computation.2 | async-start | bytes 4194304 | tf_op jit(solution)/shard_map/all_to_all | solution.py:21
  178.3 3.4 %collective-permute-start.4 = (bf16[2,16,128]{1,2,0:T(8,128)(2,1)S(1)}, bf16[2,16,128]{1,2,0:T(8,128)(2,1)S(1)}, u32[]{:S(2)}, u32[]{:S(2)}) collective-permute-start(bf16[2,16,128]{1,2,0:T(8,128)(2,1)S(1)} %get-tuple-element.28), channel_id=1, source_target_pairs={{0,32},{32,64},{64,96},{96,128},{128,160},{160,192},{192,224},{1,3... | collective-permute-start | bytes 24584 | tf_op jit(solution)/shard_map/ppermute | solution.py:60
  181.7 1.3 collective-permute-start.5
  183.0 39.1 %collective-permute-done.4 = bf16[2,16,128]{1,2,0:T(8,128)(2,1)S(1)} collective-permute-done((bf16[2,16,128]{1,2,0:T(8,128)(2,1)S(1)}, bf16[2,16,128]{1,2,0:T(8,128)(2,1)S(1)}, u32[]{:S(2)}, u32[]{:S(2)}) %collective-permute-start.4) | collective-permute-done | bytes 8224 | tf_op jit(solution)/shard_map/ppermute | solution.py:60
  222.0 4.6 %collective-permute-done.5 = bf16[2,16,128]{1,2,0:T(8,128)(2,1)S(1)} collective-permute-done((bf16[2,16,128]{1,2,0:T(8,128)(2,1)S(1)}, bf16[2,16,128]{1,2,0:T(8,128)(2,1)S(1)}, u32[]{:S(2)}, u32[]{:S(2)}) %collective-permute-start.5) | collective-permute-done | bytes 8224 | tf_op jit(solution)/shard_map/ppermute | solution.py:62
  226.7 6.6 %collective-permute-start.6 = (bf16[2,544,16]{1,2,0:T(8,128)(2,1)S(1)}, bf16[2,544,16]{1,2,0:T(8,128)(2,1)S(1)}, u32[]{:S(2)}, u32[]{:S(2)}) collective-permute-start(bf16[2,544,16]{1,2,0:T(8,128)(2,1)S(1)} %get-tuple-element.24), channel_id=1, source_target_pairs={{0,1},{1,2},{2,3},{3,4},{4,5},{5,6},{6,7},{7,8},{8,9},{9,10},{10,1... | collective-permute-start | bytes 104456 | tf_op jit(solution)/shard_map/ppermute | solution.py:60
  233.3 2.1 collective-permute-start.7
  235.4 5.3 %collective-permute-done.7 = bf16[2,544,16]{1,2,0:T(8,128)(2,1)S(1)} collective-permute-done((bf16[2,544,16]{1,2,0:T(8,128)(2,1)S(1)}, bf16[2,544,16]{1,2,0:T(8,128)(2,1)S(1)}, u32[]{:S(2)}, u32[]{:S(2)}) %collective-permute-start.7) | collective-permute-done | bytes 34848 | tf_op jit(solution)/shard_map/ppermute | solution.py:62
  241.0 4.6 %select_add_fusion = f32[2,512,128]{1,2,0:T(8,128)} fusion(f32[2,544,160]{1,2,0:T(8,128)S(1)} %maximum_convert_fusion.1, s32[]{:T(128)S(6)} %select_n.358, s32[]{:T(128)S(6)} %select_n.359, s32[]{:T(128)S(6)} %select_n.351, s32[]{:T(128)S(6)} %select_n.352, s32[]{:T(128)S(6)} %select_n.344, s32[]{:T(128)S(6)} %select_n.345, s32[]{:T(128)S(6)} %select_n.337, ...), kind=kLoop, calls=%fused_computation.34 | loop fusion | flops 5242880 | bytes 9437256 | tf_op jit(solution)/shard_map/add | solution.py:92
  245.6 4.1 %fusion.2 = f32[512,128]{0,1:T(8,128)} fusion(bf16[4096,128]{1,0:T(8,128)(2,1)} %bitcast.106, bf16[1024,4096]{0,1:T(8,128)(2,1)} %all-gather.8.cloned.1.call-done), kind=kOutput, calls=%fused_computation.2 | convolution fusion | flops 536870912 | bytes 5505024 | tf_op jit(solution)/shard_map/dot_general | solution.py:122
  249.7 4.5 %fusion.17 = f32[512,128]{0,1:T(8,128)} fusion(f32[512,128]{0,1:T(8,128)S(1)} %copy.16, f32[512,128]{0,1:T(8,128)S(1)} %copy-done.6, f32[512,128]{0,1:T(8,128)} %fusion.2, bf16[512,4096]{1,0:T(8,128)(2,1)} %all-gather.4.cloned.1.call-done, bf16[4096,256]{1,0:T(8,128)(2,1)S(1)} %bitcast.99, f32[2,512,128]{1,2,0:T(8,128)S(1)} %copy-done.8, f32[]{:T(128)S(6)} %div.4), kind=kOutput, calls=%fused_computation.21 | convolution fusion | flops 537264128 | bytes 6553604 | tf_op jit(solution)/shard_map/dot_general | solution.py:118
  254.1 1.8 copy.19
  255.9 3.4 %fusion = f32[512,128]{0,1:T(8,128)S(1)} fusion(bf16[4096,128]{1,0:T(8,128)(2,1)} %bitcast.107, bf16[1024,4096]{0,1:T(8,128)(2,1)} %all-gather.8.cloned.1.call-done), kind=kOutput, calls=%fused_computation | convolution fusion | flops 536870912 | bytes 5505024 | tf_op jit(solution)/shard_map/dot_general | solution.py:121
  259.7 1.5 fusion.23
  261.3 0.8 copy.20
  (83 shorter events, 8.4 us)
Async XLA Ops:
  7.2 24.0 %copy-start.12 = (s32[8]{0:T(128)S(1)}, s32[8]{0:T(128)}, u32[]{:S(2)}) copy-start(s32[8]{0:T(128)} %param.10) | copy-start | bytes 100
  7.2 27.3 %copy-start.11 = (f32[8,4096]{1,0:T(8,128)S(1)}, f32[8,4096]{1,0:T(8,128)}, u32[]{:S(2)}) copy-start(f32[8,4096]{1,0:T(8,128)} %param.9) | copy-start | bytes 393220
  7.2 146.9 %all-gather.6.cloned.1.call-start = ((), (), s32[]{:S(2)}) async-start(), calls=%async_computation.4 | async-start | bytes 8650752 | tf_op jit(solution)/shard_map/all_gather | solution.py:45
  10.8 147.4 %all-gather.4.cloned.1.call-start = ((), (), s32[]{:S(2)}) async-start(), calls=%async_computation.3 | async-start | bytes 4325376 | tf_op jit(solution)/shard_map/all_gather | solution.py:114
  14.4 98.6 %collective-permute-start = (bf16[2,16,128]{1,2,0:T(8,128)(2,1)}, bf16[2,16,128]{1,2,0:T(8,128)(2,1)S(1)}, u32[]{:S(2)}, u32[]{:S(2)}) collective-permute-start(bf16[2,16,128]{1,2,0:T(8,128)(2,1)} %get-tuple-element.32), channel_id=1, source_target_pairs={{0,32},{32,64},{64,96},{96,128},{128,160},{160,192},{192,224},{1,3... | collective-permute-start | bytes 24584 | tf_op jit(solution)/shard_map/ppermute | solution.py:60
  18.0 95.0 %collective-permute-start.1 = (bf16[2,16,128]{1,2,0:T(8,128)(2,1)}, bf16[2,16,128]{1,2,0:T(8,128)(2,1)S(1)}, u32[]{:S(2)}, u32[]{:S(2)}) collective-permute-start(bf16[2,16,128]{1,2,0:T(8,128)(2,1)} %get-tuple-element.33), channel_id=1, source_target_pairs={{32,0},{64,32},{96,64},{128,96},{160,128},{192,160},{224,192},{33,... | collective-permute-start | bytes 24584 | tf_op jit(solution)/shard_map/ppermute | solution.py:62
  21.3 58.1 %all-to-all-start.1 = ((bf16[8,512,128]{2,1,0:T(8,128)(2,1)}), bf16[8,512,128]{2,1,0:T(8,128)(2,1)S(1)}, u32[]{:S(2)}, u32[]{:S(2)}) async-start(bf16[8,512,128]{2,1,0:T(8,128)(2,1)} %broadcast_in_dim.49), calls=%async_computation.1 | async-start | bytes 2097152 | tf_op jit(solution)/shard_map/all_to_all | solution.py:21
  79.4 1.6 copy-start.9
  81.1 77.0 %all-to-all-start = ((bf16[8,512,256]{2,1,0:T(8,128)(2,1)}), bf16[8,512,256]{2,1,0:T(8,128)(2,1)S(1)}, u32[]{:S(2)}, u32[]{:S(2)}) async-start(bf16[8,512,256]{2,1,0:T(8,128)(2,1)} %broadcast_in_dim.48), calls=%async_computation | async-start | bytes 4194304 | tf_op jit(solution)/shard_map/all_to_all | solution.py:21
  85.2 160.4 %all-gather.8.cloned.1.call-start = ((), (), s32[]{:S(2)}) async-start(), calls=%async_computation.5 | async-start | bytes 8650752 | tf_op jit(solution)/shard_map/all_gather | solution.py:45
  98.4 63.6 %copy-start.2 = (f32[512,128]{0,1:T(8,128)}, f32[512,128]{0,1:T(8,128)S(1)}, u32[]{:S(2)}) copy-start(f32[512,128]{0,1:T(8,128)S(1)} %get-tuple-element.59) | copy-start | bytes 786436
  113.7 34.8 %collective-permute-start.2 = (bf16[2,544,16]{1,2,0:T(8,128)(2,1)}, bf16[2,544,16]{1,2,0:T(8,128)(2,1)}, u32[]{:S(2)}, u32[]{:S(2)}) collective-permute-start(bf16[2,544,16]{1,2,0:T(8,128)(2,1)} %get-tuple-element.26), channel_id=1, source_target_pairs={{0,1},{1,2},{2,3},{3,4},{4,5},{5,6},{6,7},{7,8},{8,9},{9,10},{10,1... | collective-permute-start | bytes 104456 | tf_op jit(solution)/shard_map/ppermute | solution.py:60
  125.4 23.1 %collective-permute-start.3 = (bf16[2,544,16]{1,2,0:T(8,128)(2,1)}, bf16[2,544,16]{1,2,0:T(8,128)(2,1)}, u32[]{:S(2)}, u32[]{:S(2)}) collective-permute-start(bf16[2,544,16]{1,2,0:T(8,128)(2,1)} %get-tuple-element.27), channel_id=1, source_target_pairs={{1,0},{2,1},{3,2},{4,3},{5,4},{6,5},{7,6},{8,7},{9,8},{10,9},{11,1... | collective-permute-start | bytes 104456 | tf_op jit(solution)/shard_map/ppermute | solution.py:62
  158.1 4.6 %copy-start.10 = (bf16[8,512,128]{2,1,0:T(8,128)(2,1)S(1)}, bf16[8,512,128]{2,1,0:T(8,128)(2,1)}, u32[]{:S(2)}) copy-start(bf16[8,512,128]{2,1,0:T(8,128)(2,1)} %copy-done.9) | copy-start | bytes 3145732
  162.0 0.7 copy-start.5
  162.8 3.9 %copy-start = (bf16[512,4096]{1,0:T(8,128)(2,1)S(1)}, bf16[512,4096]{1,0:T(8,128)(2,1)}, u32[]{:S(2)}) copy-start(bf16[512,4096]{1,0:T(8,128)(2,1)} %all-gather.4.cloned.1.call-done) | copy-start | bytes 12582916
  162.8 3.9 %copy-start.7 = (f32[2,512,128]{1,2,0:T(8,128)S(1)}, f32[2,512,128]{1,2,0:T(8,128)}, u32[]{:S(2)}) copy-start(f32[2,512,128]{1,2,0:T(8,128)} %select_add_fusion.1) | copy-start | bytes 1572868
  168.2 0.7 copy-start.3
  171.3 78.4 %all-to-all-start.2 = ((bf16[8,512,256]{2,1,0:T(8,128)(2,1)}), bf16[8,512,256]{2,1,0:T(8,128)(2,1)S(1)}, u32[]{:S(2)}, u32[]{:S(2)}) async-start(bf16[8,512,256]{2,1,0:T(8,128)(2,1)} %broadcast_in_dim.53), calls=%async_computation.2 | async-start | bytes 4194304 | tf_op jit(solution)/shard_map/all_to_all | solution.py:21
  178.3 43.7 %collective-permute-start.4 = (bf16[2,16,128]{1,2,0:T(8,128)(2,1)S(1)}, bf16[2,16,128]{1,2,0:T(8,128)(2,1)S(1)}, u32[]{:S(2)}, u32[]{:S(2)}) collective-permute-start(bf16[2,16,128]{1,2,0:T(8,128)(2,1)S(1)} %get-tuple-element.28), channel_id=1, source_target_pairs={{0,32},{32,64},{64,96},{96,128},{128,160},{160,192},{192,224},{1,3... | collective-permute-start | bytes 24584 | tf_op jit(solution)/shard_map/ppermute | solution.py:60
  181.7 44.9 %collective-permute-start.5 = (bf16[2,16,128]{1,2,0:T(8,128)(2,1)S(1)}, bf16[2,16,128]{1,2,0:T(8,128)(2,1)S(1)}, u32[]{:S(2)}, u32[]{:S(2)}) collective-permute-start(bf16[2,16,128]{1,2,0:T(8,128)(2,1)S(1)} %get-tuple-element.29), channel_id=1, source_target_pairs={{32,0},{64,32},{96,64},{128,96},{160,128},{192,160},{224,192},{33,... | collective-permute-start | bytes 24584 | tf_op jit(solution)/shard_map/ppermute | solution.py:62
  226.7 8.7 %collective-permute-start.6 = (bf16[2,544,16]{1,2,0:T(8,128)(2,1)S(1)}, bf16[2,544,16]{1,2,0:T(8,128)(2,1)S(1)}, u32[]{:S(2)}, u32[]{:S(2)}) collective-permute-start(bf16[2,544,16]{1,2,0:T(8,128)(2,1)S(1)} %get-tuple-element.24), channel_id=1, source_target_pairs={{0,1},{1,2},{2,3},{3,4},{4,5},{5,6},{6,7},{7,8},{8,9},{9,10},{10,1... | collective-permute-start | bytes 104456 | tf_op jit(solution)/shard_map/ppermute | solution.py:60
  233.3 7.4 %collective-permute-start.7 = (bf16[2,544,16]{1,2,0:T(8,128)(2,1)S(1)}, bf16[2,544,16]{1,2,0:T(8,128)(2,1)S(1)}, u32[]{:S(2)}, u32[]{:S(2)}) collective-permute-start(bf16[2,544,16]{1,2,0:T(8,128)(2,1)S(1)} %get-tuple-element.25), channel_id=1, source_target_pairs={{1,0},{2,1},{3,2},{4,3},{5,4},{6,5},{7,6},{8,7},{9,8},{10,9},{11,1... | collective-permute-start | bytes 104456 | tf_op jit(solution)/shard_map/ppermute | solution.py:62
  245.6 4.1 %copy-start.6 = (f32[512,128]{0,1:T(8,128)S(1)}, f32[512,128]{0,1:T(8,128)}, u32[]{:S(2)}) copy-start(f32[512,128]{0,1:T(8,128)} %copy-done.5) | copy-start | bytes 786436
  245.6 4.1 %copy-start.8 = (f32[2,512,128]{1,2,0:T(8,128)S(1)}, f32[2,512,128]{1,2,0:T(8,128)}, u32[]{:S(2)}) copy-start(f32[2,512,128]{1,2,0:T(8,128)} %select_add_fusion) | copy-start | bytes 1572868
  255.9 3.8 %copy-start.1 = (bf16[512,4096]{1,0:T(8,128)(2,1)S(1)}, bf16[512,4096]{1,0:T(8,128)(2,1)}, u32[]{:S(2)}) copy-start(bf16[512,4096]{1,0:T(8,128)(2,1)} %all-gather.4.cloned.1.call-done) | copy-start | bytes 12582916
  255.9 3.8 %copy-start.4 = (f32[512,128]{0,1:T(8,128)S(1)}, f32[512,128]{0,1:T(8,128)}, u32[]{:S(2)}) copy-start(f32[512,128]{0,1:T(8,128)} %copy-done.3) | copy-start | bytes 786436
Sparse Core Ops, SparseCore 0:
  11.0 66.5 all-gather.5
  80.1 53.4 all-gather.3
  169.8 58.7 all-gather.7
where the time goes:
time: 270 us; the launch traced here: 269 us
  starting transfers between devices  52.8 us (20%)
  waiting for transfers between devices  49.7 us (18%)
  blocking collectives  46.5 us (17%)
  between operations  40.8 us (15%)
  other arithmetic  29.7 us (11%)
  matrix products  26.7 us (10%)
  local copies, waits for them, and re-layouts  22.4 us (8%)
    psum x4, blocking collectives, by_axis(): x = lax.psum(x, axis)  46.5 us
    ppermute x4, waiting for transfers between devices, extended(): lax.ppermute(tail, axis, [(i, (i + 1) % count) for i in range(ends)])  39.1 us
    ppermute x4, starting transfers between devices, extended(): lax.ppermute(tail, axis, [(i, (i + 1) % count) for i in range(ends)])  25.2 us
    all_to_all x3, starting transfers between devices, sent_to_all(): lax.all_to_all(jnp.broadcast_to(x[None], (peers, *x.shape)), axis, 0, 0,...  20.9 us
    ppermute x4, waiting for transfers between devices, extended(): lax.ppermute(head, axis, [((i + 1) % count, i) for i in range(ends)])  9.9 us
    add x2, other arithmetic, dissipate(): summed = summed + jnp.where(jump_slot < active, contribution, 0.0)  9.16 us
    dot_general x2, matrix products, drift(): left_imag = jnp.dot(strip, pieces[1], preferred_element_type=jnp.float32)  8.3 us
    dot_general x2, matrix products, drift(): right_imag = jnp.dot(pieces[1], strip, preferred_element_type=jnp.float32)  8.05 us
  transfers between devices with their start and end apart: 14, of which 3 were waited for; matrix products, arithmetic and copies ran while one was open for 19% of the time, Pallas kernels for 0%

commit v1 on v0

--- a/solution.py
+++ b/solution.py
@@ -8,6 +8,12 @@
 COL = ("col_0", "col_1", "col_2")
 ROW_COL = ("row", "col_0", "col_1", "col_2")
 step_size = 0.25
+
+
+def summed_here(shard, mesh_axis):
+    parts = lax.all_gather(shard, mesh_axis, axis=0, tiled=False)
+    total = parts.sum(axis=0)
+    return total
 
 
 def in_order(tiles, dim):
@@ -27,7 +33,7 @@
 
 def by_axis(x, axes):
     for axis in axes:
-        x = lax.psum(x, axis)
+        x = summed_here(x, axis)
     return x
 
 

time: 270 us -> 289 us (1.070)
  local copies, waits for them, and re-layouts: 22.4 us -> 40.6 us
  other arithmetic: 29.7 us -> 35.2 us
  blocking collectives: 46.5 us -> 42 us
    psum x4 -> x0, blocking collectives: 46.5 us -> none  [by_axis(): x = lax.psum(x, axis)]
    unnamed x0 -> x4, blocking collectives: none -> 42 us
    unnamed x30 -> x50, local copies, waits for them, and re-layouts: 6.65 us -> 15.9 us
    dynamic_slice x8, local copies, waits for them, and re-layouts: 0.59 us -> 5.15 us  [dissipate(): row_strength = lax.dynamic_slice_in_dim(strength, row_first, height)]
    dynamic_slice x8, local copies, waits for them, and re-layouts: 0.6 us -> 4.92 us  [dissipate(): col_strength = lax.dynamic_slice_in_dim(strength, col_first, breadth)]
  transfers between devices with their start and end apart: 14 -> 14, of which waited for: 3 -> 3; matrix products, arithmetic and copies ran while one was open for 19% -> 26% of each run, Pallas kernels for 0% -> 0%
where the time goes in v1:
time: 289 us; the launch traced here: 288 us
  starting transfers between devices  52.4 us (18%)
  waiting for transfers between devices  49.8 us (17%)
  blocking collectives  42 us (15%)
  between operations  41.2 us (14%)
  local copies, waits for them, and re-layouts  40.6 us (14%)
  other arithmetic  35.2 us (12%)
  matrix products  26.7 us (9%)
    unnamed x4, blocking collectives  42 us
    ppermute x4, waiting for transfers between devices, extended(): lax.ppermute(tail, axis, [(i, (i + 1) % count) for i in range(ends)])  39 us
    ppermute x4, starting transfers between devices, extended(): lax.ppermute(tail, axis, [(i, (i + 1) % count) for i in range(ends)])  24.8 us
    all_to_all x3, starting transfers between devices, sent_to_all(): lax.all_to_all(jnp.broadcast_to(x[None], (peers, *x.shape)), axis, 0, 0,...  20.9 us
    unnamed x50, local copies, waits for them, and re-layouts  15.9 us
    ppermute x4, waiting for transfers between devices, extended(): lax.ppermute(head, axis, [((i + 1) % count, i) for i in range(ends)])  9.92 us
    add x2, other arithmetic, dissipate(): summed = summed + jnp.where(jump_slot < active, contribution, 0.0)  9.19 us
    dot_general x2, matrix products, drift(): left_imag = jnp.dot(strip, pieces[1], preferred_element_type=jnp.float32)  8.3 us
  transfers between devices with their start and end apart: 14, of which 3 were waited for; matrix products, arithmetic and copies ran while one was open for 26% of the time, Pallas kernels for 0%

profile of v1, /device:TPU:25, one launch (start us, length us, event | category | flops | bytes accessed | tf_op | source)
XLA Modules:
  0.0 287.8 jit_solution(1842468939118752620)
XLA Ops:
  7.3 1.0 convert_element_type.42
  8.3 1.8 select_reduce_fusion
  10.0 0.7 pad_maximum_fusion.3
  10.8 0.7 all-gather.4.cloned.1.call-update
  11.5 1.1 copy.16
  12.6 1.1 copy.10
  13.7 0.7 fusion.83
  14.5 3.5 %collective-permute-start = (bf16[2,16,128]{1,2,0:T(8,128)(2,1)}, bf16[2,16,128]{1,2,0:T(8,128)(2,1)S(1)}, u32[]{:S(2)}, u32[]{:S(2)}) collective-permute-start(bf16[2,16,128]{1,2,0:T(8,128)(2,1)} %get-tuple-element.32), channel_id=1, source_target_pairs={{0,32},{32,64},{64,96},{96,128},{128,160},{160,192},{192,224},{1,3... | collective-permute-start | bytes 24584 | tf_op jit(solution)/shard_map/ppermute | solution.py:66
  18.0 1.3 collective-permute-start.1
  19.3 2.0 broadcast_in_dim.49
  21.3 9.8 %all-to-all-start.1 = ((bf16[8,512,128]{2,1,0:T(8,128)(2,1)}), bf16[8,512,128]{2,1,0:T(8,128)(2,1)S(1)}, u32[]{:S(2)}, u32[]{:S(2)}) async-start(bf16[8,512,128]{2,1,0:T(8,128)(2,1)} %broadcast_in_dim.49), calls=%async_computation.1 | async-start | bytes 2097152 | tf_op jit(solution)/shard_map/all_to_all | solution.py:27
  31.2 0.7 fusion.85
  34.5 0.7 dynamic-slice
  35.2 1.4 dynamic-update-slice
  38.0 0.7 fusion.66
  38.7 0.7 fusion.72
  40.7 25.0 %all-reduce.8 = f32[8]{0:T(128)S(1)} all-reduce(f32[8]{0:T(128)S(1)} %dynamic-update-slice), channel_id=1, replica_groups=mesh['row'=8,'col_0'=4,'col_1'=4,'col_2'=2] {'row'}, use_global_device_ids=true, to_apply=%add.8 | all-reduce | flops 8 | bytes 64
  73.2 1.4 dynamic-update-slice.1
  80.3 0.7 fusion.78
  81.7 1.5 broadcast_in_dim.48
  83.3 4.2 %all-to-all-start = ((bf16[8,512,256]{2,1,0:T(8,128)(2,1)}), bf16[8,512,256]{2,1,0:T(8,128)(2,1)S(1)}, u32[]{:S(2)}, u32[]{:S(2)}) async-start(bf16[8,512,256]{2,1,0:T(8,128)(2,1)} %broadcast_in_dim.48), calls=%async_computation | async-start | bytes 4194304 | tf_op jit(solution)/shard_map/all_to_all | solution.py:27
  88.1 8.3 %all-reduce.9 = f32[4]{0:T(128)S(1)} all-reduce(f32[4]{0:T(128)S(1)} %dynamic-update-slice.1), channel_id=1, replica_groups=mesh['row'=8,'col_0'=4,'col_1'=4,'col_2'=2] {'col_0'}, use_global_device_ids=true, to_apply=%add.9 | all-reduce | flops 4 | bytes 32
  109.1 1.5 dynamic-update-slice.2
  111.9 0.8 broadcast_multiply_fusion
  112.7 1.5 add_multiply_fusion.2
  114.2 1.6 broadcast_multiply_fusion.6
  115.8 1.6 add_multiply_fusion.8
  117.4 1.6 broadcast_multiply_fusion.4
  119.0 1.6 add_multiply_fusion.6
  120.6 1.6 broadcast_multiply_fusion.2
  122.8 6.2 %all-reduce.10 = f32[4]{0:T(128)S(1)} all-reduce(f32[4]{0:T(128)} %copy-done.16), channel_id=1, replica_groups=mesh['row'=8,'col_0'=4,'col_1'=4,'col_2'=2] {'col_1'}, use_global_device_ids=true, to_apply=%add.10 | all-reduce | flops 4 | bytes 32
  129.1 1.3 dynamic-slice.3
  131.0 1.3 dynamic-update-slice.3
  132.3 0.7 pad_maximum_fusion.11
  133.0 11.3 %collective-permute-start.2 = (bf16[2,544,16]{1,2,0:T(8,128)(2,1)}, bf16[2,544,16]{1,2,0:T(8,128)(2,1)}, u32[]{:S(2)}, u32[]{:S(2)}) collective-permute-start(bf16[2,544,16]{1,2,0:T(8,128)(2,1)} %get-tuple-element.26), channel_id=1, source_target_pairs={{0,1},{1,2},{2,3},{3,4},{4,5},{5,6},{6,7},{7,8},{8,9},{9,10},{10,1... | collective-permute-start | bytes 104456 | tf_op jit(solution)/shard_map/ppermute | solution.py:66
  144.3 1.9 collective-permute-start.3
  146.2 1.6 add_multiply_fusion.4
  147.8 2.5 all-reduce.11
  166.2 0.7 reduce_sum.49
  167.7 1.0 maximum_convert_fusion
  168.7 4.6 %select_add_fusion.1 = f32[2,512,128]{1,2,0:T(8,128)} fusion(f32[2,544,160]{1,2,0:T(8,128)S(1)} %maximum_convert_fusion, s32[]{:T(128)S(6)} %select_n.358, s32[]{:T(128)S(6)} %select_n.359, s32[]{:T(128)S(6)} %select_n.351, s32[]{:T(128)S(6)} %select_n.352, s32[]{:T(128)S(6)} %select_n.344, s32[]{:T(128)S(6)} %select_n.345, s32[]{:T(128)S(6)} %select_n.337, ...), kind=kLoop, calls=%fused_computation.35 | loop fusion | flops 5242880 | bytes 9437256 | tf_op jit(solution)/shard_map/add | solution.py:98
  173.2 4.0 %fusion.6 = f32[512,128]{0,1:T(8,128)S(1)} fusion(bf16[4096,128]{1,0:T(8,128)(2,1)} %bitcast.113, bf16[1024,4096]{1,0:T(8,128)(2,1)} %all-gather.6.cloned.1.call-done), kind=kOutput, calls=%fused_computation.6 | convolution fusion | flops 536870912 | bytes 5505024 | tf_op jit(solution)/shard_map/dot_general | solution.py:128
  177.3 3.8 %fusion.9 = f32[512,128]{0,1:T(8,128)S(1)} fusion(f32[512,128]{0,1:T(8,128)S(1)} %fusion.6, bf16[512,4096]{1,0:T(8,128)(2,1)} %all-gather.4.cloned.1.call-done, bf16[4096,256]{1,0:T(8,128)(2,1)S(1)} %bitcast.105, f32[2,512,128]{1,2,0:T(8,128)} %select_add_fusion.1), kind=kOutput, calls=%fused_computation.13 | convolution fusion | flops 537001984 | bytes 6029312 | tf_op jit(solution)/shard_map/dot_general | solution.py:124
  181.1 0.7 copy-done.5
  181.9 3.8 %fusion.4 = f32[512,128]{0,1:T(8,128)S(1)} fusion(bf16[4096,128]{1,0:T(8,128)(2,1)S(1)} %bitcast.116, bf16[1024,4096]{1,0:T(8,128)(2,1)} %all-gather.6.cloned.1.call-done), kind=kOutput, calls=%fused_computation.4 | convolution fusion | flops 536870912 | bytes 5505024 | tf_op jit(solution)/shard_map/dot_general | solution.py:127
  185.8 1.5 fusion.11
  187.3 0.7 copy-done.3
  188.0 0.7 pad_maximum_fusion.5
  189.0 1.4 broadcast_in_dim.53
  190.4 6.9 %all-to-all-start.2 = ((bf16[8,512,256]{2,1,0:T(8,128)(2,1)}), bf16[8,512,256]{2,1,0:T(8,128)(2,1)S(1)}, u32[]{:S(2)}, u32[]{:S(2)}) async-start(bf16[8,512,256]{2,1,0:T(8,128)(2,1)} %broadcast_in_dim.53), calls=%async_computation.2 | async-start | bytes 4194304 | tf_op jit(solution)/shard_map/all_to_all | solution.py:27
  197.4 3.4 %collective-permute-start.4 = (bf16[2,16,128]{1,2,0:T(8,128)(2,1)S(1)}, bf16[2,16,128]{1,2,0:T(8,128)(2,1)S(1)}, u32[]{:S(2)}, u32[]{:S(2)}) collective-permute-start(bf16[2,16,128]{1,2,0:T(8,128)(2,1)S(1)} %get-tuple-element.28), channel_id=1, source_target_pairs={{0,32},{32,64},{64,96},{96,128},{128,160},{160,192},{192,224},{1,3... | collective-permute-start | bytes 24584 | tf_op jit(solution)/shard_map/ppermute | solution.py:66
  200.8 1.3 collective-permute-start.5
  202.1 39.0 %collective-permute-done.4 = bf16[2,16,128]{1,2,0:T(8,128)(2,1)S(1)} collective-permute-done((bf16[2,16,128]{1,2,0:T(8,128)(2,1)S(1)}, bf16[2,16,128]{1,2,0:T(8,128)(2,1)S(1)}, u32[]{:S(2)}, u32[]{:S(2)}) %collective-permute-start.4) | collective-permute-done | bytes 8224 | tf_op jit(solution)/shard_map/ppermute | solution.py:66
  241.1 4.6 %collective-permute-done.5 = bf16[2,16,128]{1,2,0:T(8,128)(2,1)S(1)} collective-permute-done((bf16[2,16,128]{1,2,0:T(8,128)(2,1)S(1)}, bf16[2,16,128]{1,2,0:T(8,128)(2,1)S(1)}, u32[]{:S(2)}, u32[]{:S(2)}) %collective-permute-start.5) | collective-permute-done | bytes 8224 | tf_op jit(solution)/shard_map/ppermute | solution.py:68
  245.8 6.6 %collective-permute-start.6 = (bf16[2,544,16]{1,2,0:T(8,128)(2,1)S(1)}, bf16[2,544,16]{1,2,0:T(8,128)(2,1)S(1)}, u32[]{:S(2)}, u32[]{:S(2)}) collective-permute-start(bf16[2,544,16]{1,2,0:T(8,128)(2,1)S(1)} %get-tuple-element.24), channel_id=1, source_target_pairs={{0,1},{1,2},{2,3},{3,4},{4,5},{5,6},{6,7},{7,8},{8,9},{9,10},{10,1... | collective-permute-start | bytes 104456 | tf_op jit(solution)/shard_map/ppermute | solution.py:66
  252.4 2.1 collective-permute-start.7
  254.6 5.3 %collective-permute-done.7 = bf16[2,544,16]{1,2,0:T(8,128)(2,1)S(1)} collective-permute-done((bf16[2,544,16]{1,2,0:T(8,128)(2,1)S(1)}, bf16[2,544,16]{1,2,0:T(8,128)(2,1)S(1)}, u32[]{:S(2)}, u32[]{:S(2)}) %collective-permute-start.7) | collective-permute-done | bytes 34848 | tf_op jit(solution)/shard_map/ppermute | solution.py:68
  260.1 4.6 %select_add_fusion = f32[2,512,128]{1,2,0:T(8,128)} fusion(f32[2,544,160]{1,2,0:T(8,128)S(1)} %maximum_convert_fusion.1, s32[]{:T(128)S(6)} %select_n.358, s32[]{:T(128)S(6)} %select_n.359, s32[]{:T(128)S(6)} %select_n.351, s32[]{:T(128)S(6)} %select_n.352, s32[]{:T(128)S(6)} %select_n.344, s32[]{:T(128)S(6)} %select_n.345, s32[]{:T(128)S(6)} %select_n.337, ...), kind=kLoop, calls=%fused_computation.34 | loop fusion | flops 5242880 | bytes 9437256 | tf_op jit(solution)/shard_map/add | solution.py:98
  264.7 4.1 %fusion.2 = f32[512,128]{0,1:T(8,128)} fusion(bf16[4096,128]{1,0:T(8,128)(2,1)} %bitcast.114, bf16[1024,4096]{0,1:T(8,128)(2,1)} %all-gather.8.cloned.1.call-done), kind=kOutput, calls=%fused_computation.2 | convolution fusion | flops 536870912 | bytes 5505024 | tf_op jit(solution)/shard_map/dot_general | solution.py:128
  268.8 4.5 %fusion.17 = f32[512,128]{0,1:T(8,128)} fusion(f32[512,128]{0,1:T(8,128)S(1)} %copy.16, f32[512,128]{0,1:T(8,128)S(1)} %copy-done.6, f32[512,128]{0,1:T(8,128)} %fusion.2, bf16[512,4096]{1,0:T(8,128)(2,1)} %all-gather.4.cloned.1.call-done, bf16[4096,256]{1,0:T(8,128)(2,1)S(1)} %bitcast.107, f32[2,512,128]{1,2,0:T(8,128)S(1)} %copy-done.8, f32[]{:T(128)S(6)} %div.4), kind=kOutput, calls=%fused_computation.21 | convolution fusion | flops 537264128 | bytes 6553604 | tf_op jit(solution)/shard_map/dot_general | solution.py:124
  273.3 1.8 copy.19
  275.1 3.4 %fusion = f32[512,128]{0,1:T(8,128)S(1)} fusion(bf16[4096,128]{1,0:T(8,128)(2,1)} %bitcast.115, bf16[1024,4096]{0,1:T(8,128)(2,1)} %all-gather.8.cloned.1.call-done), kind=kOutput, calls=%fused_computation | convolution fusion | flops 536870912 | bytes 5505024 | tf_op jit(solution)/shard_map/dot_general | solution.py:127
  278.8 1.5 fusion.23
  280.4 0.8 copy.20
  (107 shorter events, 26.0 us)
Async XLA Ops:
  7.2 27.3 %copy-start.15 = (u32[256]{0:T(256)S(1)}, u32[256]{0:T(256)}, u32[]{:S(2)}) copy-start(u32[256]{0:T(256)} %constant.180) | copy-start | bytes 3076
  7.2 64.7 %copy-start.14 = (u32[256]{0:T(256)S(1)}, u32[256]{0:T(256)}, u32[]{:S(2)}) copy-start(u32[256]{0:T(256)} %constant.185) | copy-start | bytes 3076
  7.2 24.0 %copy-start.12 = (s32[8]{0:T(128)S(1)}, s32[8]{0:T(128)}, u32[]{:S(2)}) copy-start(s32[8]{0:T(128)} %param.10) | copy-start | bytes 100
  7.2 29.4 %copy-start.11 = (f32[8,4096]{1,0:T(8,128)S(1)}, f32[8,4096]{1,0:T(8,128)}, u32[]{:S(2)}) copy-start(f32[8,4096]{1,0:T(8,128)} %param.9) | copy-start | bytes 393220
  7.2 166.0 %all-gather.6.cloned.1.call-start = ((), (), s32[]{:S(2)}) async-start(), calls=%async_computation.4 | async-start | bytes 8650752 | tf_op jit(solution)/shard_map/all_gather | solution.py:51
  10.8 166.5 %all-gather.4.cloned.1.call-start = ((), (), s32[]{:S(2)}) async-start(), calls=%async_computation.3 | async-start | bytes 4325376 | tf_op jit(solution)/shard_map/all_gather | solution.py:120
  14.5 117.8 %collective-permute-start = (bf16[2,16,128]{1,2,0:T(8,128)(2,1)}, bf16[2,16,128]{1,2,0:T(8,128)(2,1)S(1)}, u32[]{:S(2)}, u32[]{:S(2)}) collective-permute-start(bf16[2,16,128]{1,2,0:T(8,128)(2,1)} %get-tuple-element.32), channel_id=1, source_target_pairs={{0,32},{32,64},{64,96},{96,128},{128,160},{160,192},{192,224},{1,3... | collective-permute-start | bytes 24584 | tf_op jit(solution)/shard_map/ppermute | solution.py:66
  18.0 114.3 %collective-permute-start.1 = (bf16[2,16,128]{1,2,0:T(8,128)(2,1)}, bf16[2,16,128]{1,2,0:T(8,128)(2,1)S(1)}, u32[]{:S(2)}, u32[]{:S(2)}) collective-permute-start(bf16[2,16,128]{1,2,0:T(8,128)(2,1)} %get-tuple-element.33), channel_id=1, source_target_pairs={{32,0},{64,32},{96,64},{128,96},{160,128},{192,160},{224,192},{33,... | collective-permute-start | bytes 24584 | tf_op jit(solution)/shard_map/ppermute | solution.py:68
  21.3 60.4 %all-to-all-start.1 = ((bf16[8,512,128]{2,1,0:T(8,128)(2,1)}), bf16[8,512,128]{2,1,0:T(8,128)(2,1)S(1)}, u32[]{:S(2)}, u32[]{:S(2)}) async-start(bf16[8,512,128]{2,1,0:T(8,128)(2,1)} %broadcast_in_dim.49), calls=%async_computation.1 | async-start | bytes 2097152 | tf_op jit(solution)/shard_map/all_to_all | solution.py:27
  31.2 76.6 %copy-start.13 = (u32[256]{0:T(256)S(1)}, u32[256]{0:T(256)}, u32[]{:S(2)}) copy-start(u32[256]{0:T(256)} %constant.190) | copy-start | bytes 3076
  81.7 1.6 copy-start.9
  83.3 93.9 %all-to-all-start = ((bf16[8,512,256]{2,1,0:T(8,128)(2,1)}), bf16[8,512,256]{2,1,0:T(8,128)(2,1)S(1)}, u32[]{:S(2)}, u32[]{:S(2)}) async-start(bf16[8,512,256]{2,1,0:T(8,128)(2,1)} %broadcast_in_dim.48), calls=%async_computation | async-start | bytes 4194304 | tf_op jit(solution)/shard_map/all_to_all | solution.py:27
  87.5 177.2 %all-gather.8.cloned.1.call-start = ((), (), s32[]{:S(2)}) async-start(), calls=%async_computation.5 | async-start | bytes 8650752 | tf_op jit(solution)/shard_map/all_gather | solution.py:51
  110.6 0.6 copy-start.16
  112.7 68.4 %copy-start.2 = (f32[512,128]{0,1:T(8,128)}, f32[512,128]{0,1:T(8,128)S(1)}, u32[]{:S(2)}) copy-start(f32[512,128]{0,1:T(8,128)S(1)} %get-tuple-element.59) | copy-start | bytes 786436
  133.0 34.6 %collective-permute-start.2 = (bf16[2,544,16]{1,2,0:T(8,128)(2,1)}, bf16[2,544,16]{1,2,0:T(8,128)(2,1)}, u32[]{:S(2)}, u32[]{:S(2)}) collective-permute-start(bf16[2,544,16]{1,2,0:T(8,128)(2,1)} %get-tuple-element.26), channel_id=1, source_target_pairs={{0,1},{1,2},{2,3},{3,4},{4,5},{5,6},{6,7},{7,8},{8,9},{9,10},{10,1... | collective-permute-start | bytes 104456 | tf_op jit(solution)/shard_map/ppermute | solution.py:66
  144.3 23.4 %collective-permute-start.3 = (bf16[2,544,16]{1,2,0:T(8,128)(2,1)}, bf16[2,544,16]{1,2,0:T(8,128)(2,1)}, u32[]{:S(2)}, u32[]{:S(2)}) collective-permute-start(bf16[2,544,16]{1,2,0:T(8,128)(2,1)} %get-tuple-element.27), channel_id=1, source_target_pairs={{1,0},{2,1},{3,2},{4,3},{5,4},{6,5},{7,6},{8,7},{9,8},{10,9},{11,1... | collective-permute-start | bytes 104456 | tf_op jit(solution)/shard_map/ppermute | solution.py:68
  177.3 4.6 %copy-start.10 = (bf16[8,512,128]{2,1,0:T(8,128)(2,1)S(1)}, bf16[8,512,128]{2,1,0:T(8,128)(2,1)}, u32[]{:S(2)}) copy-start(bf16[8,512,128]{2,1,0:T(8,128)(2,1)} %copy-done.9) | copy-start | bytes 3145732
  181.1 0.7 copy-start.5
  181.9 3.9 %copy-start = (bf16[512,4096]{1,0:T(8,128)(2,1)S(1)}, bf16[512,4096]{1,0:T(8,128)(2,1)}, u32[]{:S(2)}) copy-start(bf16[512,4096]{1,0:T(8,128)(2,1)} %all-gather.4.cloned.1.call-done) | copy-start | bytes 12582916
  181.9 3.9 %copy-start.7 = (f32[2,512,128]{1,2,0:T(8,128)S(1)}, f32[2,512,128]{1,2,0:T(8,128)}, u32[]{:S(2)}) copy-start(f32[2,512,128]{1,2,0:T(8,128)} %select_add_fusion.1) | copy-start | bytes 1572868
  187.3 0.7 copy-start.3
  190.4 78.4 %all-to-all-start.2 = ((bf16[8,512,256]{2,1,0:T(8,128)(2,1)}), bf16[8,512,256]{2,1,0:T(8,128)(2,1)S(1)}, u32[]{:S(2)}, u32[]{:S(2)}) async-start(bf16[8,512,256]{2,1,0:T(8,128)(2,1)} %broadcast_in_dim.53), calls=%async_computation.2 | async-start | bytes 4194304 | tf_op jit(solution)/shard_map/all_to_all | solution.py:27
  197.4 43.7 %collective-permute-start.4 = (bf16[2,16,128]{1,2,0:T(8,128)(2,1)S(1)}, bf16[2,16,128]{1,2,0:T(8,128)(2,1)S(1)}, u32[]{:S(2)}, u32[]{:S(2)}) collective-permute-start(bf16[2,16,128]{1,2,0:T(8,128)(2,1)S(1)} %get-tuple-element.28), channel_id=1, source_target_pairs={{0,32},{32,64},{64,96},{96,128},{128,160},{160,192},{192,224},{1,3... | collective-permute-start | bytes 24584 | tf_op jit(solution)/shard_map/ppermute | solution.py:66
  200.8 44.9 %collective-permute-start.5 = (bf16[2,16,128]{1,2,0:T(8,128)(2,1)S(1)}, bf16[2,16,128]{1,2,0:T(8,128)(2,1)S(1)}, u32[]{:S(2)}, u32[]{:S(2)}) collective-permute-start(bf16[2,16,128]{1,2,0:T(8,128)(2,1)S(1)} %get-tuple-element.29), channel_id=1, source_target_pairs={{32,0},{64,32},{96,64},{128,96},{160,128},{192,160},{224,192},{33,... | collective-permute-start | bytes 24584 | tf_op jit(solution)/shard_map/ppermute | solution.py:68
  245.8 8.7 %collective-permute-start.6 = (bf16[2,544,16]{1,2,0:T(8,128)(2,1)S(1)}, bf16[2,544,16]{1,2,0:T(8,128)(2,1)S(1)}, u32[]{:S(2)}, u32[]{:S(2)}) collective-permute-start(bf16[2,544,16]{1,2,0:T(8,128)(2,1)S(1)} %get-tuple-element.24), channel_id=1, source_target_pairs={{0,1},{1,2},{2,3},{3,4},{4,5},{5,6},{6,7},{7,8},{8,9},{9,10},{10,1... | collective-permute-start | bytes 104456 | tf_op jit(solution)/shard_map/ppermute | solution.py:66
  252.4 7.4 %collective-permute-start.7 = (bf16[2,544,16]{1,2,0:T(8,128)(2,1)S(1)}, bf16[2,544,16]{1,2,0:T(8,128)(2,1)S(1)}, u32[]{:S(2)}, u32[]{:S(2)}) collective-permute-start(bf16[2,544,16]{1,2,0:T(8,128)(2,1)S(1)} %get-tuple-element.25), channel_id=1, source_target_pairs={{1,0},{2,1},{3,2},{4,3},{5,4},{6,5},{7,6},{8,7},{9,8},{10,9},{11,1... | collective-permute-start | bytes 104456 | tf_op jit(solution)/shard_map/ppermute | solution.py:68
  264.7 4.1 %copy-start.6 = (f32[512,128]{0,1:T(8,128)S(1)}, f32[512,128]{0,1:T(8,128)}, u32[]{:S(2)}) copy-start(f32[512,128]{0,1:T(8,128)} %copy-done.5) | copy-start | bytes 786436
  264.7 4.1 %copy-start.8 = (f32[2,512,128]{1,2,0:T(8,128)S(1)}, f32[2,512,128]{1,2,0:T(8,128)}, u32[]{:S(2)}) copy-start(f32[2,512,128]{1,2,0:T(8,128)} %select_add_fusion) | copy-start | bytes 1572868
  275.1 3.8 %copy-start.1 = (bf16[512,4096]{1,0:T(8,128)(2,1)S(1)}, bf16[512,4096]{1,0:T(8,128)(2,1)}, u32[]{:S(2)}) copy-start(bf16[512,4096]{1,0:T(8,128)(2,1)} %all-gather.4.cloned.1.call-done) | copy-start | bytes 12582916
  275.1 3.8 %copy-start.4 = (f32[512,128]{0,1:T(8,128)S(1)}, f32[512,128]{0,1:T(8,128)}, u32[]{:S(2)}) copy-start(f32[512,128]{0,1:T(8,128)} %copy-done.3) | copy-start | bytes 786436
Sparse Core Ops, SparseCore 0:
  11.1 66.5 all-gather.5
  80.1 53.4 all-gather.3
  188.9 58.7 all-gather.7
